TPU v7x, 32 devices: a whole 2x2x4 slice. The times are simulated.
32 devices in a mesh: src: 8 (over z, x), rcv: 4 (over y, core).
Axes of the slice: x: 2, y: 2, z: 4, core: 2. Of those that a mesh axis runs over, the one named last changes fastest.
Arguments:
- traces: bfloat16 [2, 2, 2048, 2048], P(None, None, 'src', 'rcv'), may hold values from -8 to 8
- wavelet: float32 [2, 2], replicated, may hold values from -0.3 to 0.3
Outputs:
- coeffs: float32 [2, 2, 2048, 2048], P(None, None, 'src', 'rcv')
- norms: float32 [2, 2], replicated
All inputs are finite; a program needn't handle non-finite values.
Results may differ from a plain program's by a relative error of at most 0.006.
Values may be sent and summed in bfloat16 or wider, within the bound.
A program may use at most 128 MiB of HBM per device.

v0:
```python
import math

import jax
import jax.numpy as jnp
from jax import lax
from jax.sharding import PartitionSpec as P

ITERS = 2


step_length = 0.4
shrink_fraction = 0.2


def table_block(offset, height, second, breadth, length, direction):
    left_index = offset + jnp.arange(height, dtype=jnp.int32)
    right_index = second + jnp.arange(breadth, dtype=jnp.int32)
    phase = left_index[:, None] * right_index[None, :] % length
    angle = phase.astype(jnp.float32) * (2.0 * math.pi / length)
    scale = 1.0 / math.sqrt(length)
    return jnp.stack([jnp.cos(angle) * scale, direction * (jnp.sin(angle) * scale)]).astype(
        jnp.bfloat16
    )


def complex_product(left_side, right_side, pattern, left_table, right_table):
    left_re = left_side[0] if left_table else left_side[:, 0]
    left_im = left_side[1] if left_table else left_side[:, 1]
    right_re = right_side[0] if right_table else right_side[:, 0]
    right_im = right_side[1] if right_table else right_side[:, 1]

    def single(first_op, second_op):
        return jnp.einsum(pattern, first_op, second_op, preferred_element_type=jnp.float32)

    real_part = single(left_re, right_re) - single(left_im, right_im)
    imag_part = single(left_re, right_im) + single(left_im, right_re)
    return jnp.stack([real_part, imag_part], axis=1)


def complex_scale(real_part, imag_part, values):
    return jnp.stack(
        [
            real_part * values[:, 0] - imag_part * values[:, 1],
            real_part * values[:, 1] + imag_part * values[:, 0],
        ],
        axis=1,
    )


def per_device(traces, wavelet):
    row_count = traces.shape[2]
    col_count = traces.shape[3]
    extent = row_count * lax.axis_size("src")
    row_anchor = lax.axis_index("src") * row_count
    col_anchor = lax.axis_index("rcv") * col_count
    root_scale = 1.0 / math.sqrt(extent)
    wave_re = (wavelet[:, 0] * root_scale)[:, None, None]
    wave_im = (wavelet[:, 1] * root_scale)[:, None, None]
    forward_cols = table_block(0, extent, col_anchor, col_count, extent, -1.0)
    forward_rows = table_block(row_anchor, row_count, 0, extent, extent, -1.0)
    inverse_cols = table_block(0, extent, col_anchor, col_count, extent, 1.0)
    inverse_rows = table_block(row_anchor, row_count, 0, extent, extent, 1.0)
    coeffs = jnp.zeros(traces.shape, jnp.float32)
    columns_all = lax.all_gather(traces, "src", axis=2, tiled=True)
    traces_f = traces.astype(jnp.float32)

    def row_section(table, portion):
        return complex_product(portion, table, "fmn,nc->fmc", False, True)

    def column_section(table, portion):
        return complex_product(table, portion, "mn,fnc->fmc", True, False)

    def paired(first_op, second_op):
        return jnp.einsum("fmr,fkr->fmk", first_op, second_op, preferred_element_type=jnp.float32)

    norm_list = []
    for iteration in range(ITERS):
        if iteration == 0:
            misfit = traces_f
        else:
            coeff_half = coeffs.astype(jnp.bfloat16)
            halfway = column_section(
                inverse_rows, lax.all_gather(coeff_half, "src", axis=2, tiled=True)
            ).astype(jnp.bfloat16)
            model = row_section(
                inverse_cols, lax.all_gather(halfway, "rcv", axis=3, tiled=True)
            ).astype(jnp.bfloat16)
            product = complex_product(
                lax.all_gather(model, "rcv", axis=3, tiled=True),
                columns_all,
                "fmn,fnc->fmc",
                False,
                False,
            )
            misfit = traces_f - model.astype(jnp.float32) + complex_scale(wave_re, wave_im, product)
        local_squares = jnp.sum(misfit * misfit, axis=(1, 2, 3))
        norm_list.append(jnp.sqrt(lax.psum(local_squares, ("src", "rcv"))))
        misfit_half = misfit.astype(jnp.bfloat16)
        misfit_re = misfit_half[:, 0]
        misfit_im = misfit_half[:, 1]
        column_re = columns_all[:, 0]
        column_im = columns_all[:, 1]
        back_re = paired(misfit_re, column_re) + paired(misfit_im, column_re * 0 + column_im)
        back_im = paired(misfit_im, column_re) - paired(misfit_re, column_im)
        scaled = complex_scale(wave_re, -wave_im, jnp.stack([back_re, back_im], axis=1))
        summed = lax.psum_scatter(
            scaled.astype(jnp.bfloat16), "rcv", scatter_dimension=3, tiled=True
        ).astype(jnp.float32)
        grad_half = (misfit_half.astype(jnp.float32) - summed).astype(jnp.bfloat16)
        halfway = row_section(
            forward_cols, lax.all_gather(grad_half, "rcv", axis=3, tiled=True)
        ).astype(jnp.bfloat16)
        spectrum = column_section(forward_rows, lax.all_gather(halfway, "src", axis=2, tiled=True))
        trial = coeffs + step_length * spectrum
        magnitude = jnp.sqrt(trial[:, 0] * trial[:, 0] + trial[:, 1] * trial[:, 1])
        local_peak = jnp.max(magnitude, axis=(1, 2))
        global_peak = lax.pmax(local_peak, ("src", "rcv"))
        level = shrink_fraction * global_peak[:, None, None]
        factor = jnp.maximum(1.0 - level / jnp.maximum(magnitude, level), 0.0)
        coeffs = trial * factor[:, None]
    return (coeffs, jnp.stack(norm_list))


def solution(mesh):
    in_specs = (P(None, None, "src", "rcv"), P())
    out_specs = (P(None, None, "src", "rcv"), P())
    return jax.shard_map(
        per_device, mesh=mesh, in_specs=in_specs, out_specs=out_specs, check_vma=False
    )
```

profile of v0, /device:TPU:14, one launch (start us, length us, event | category | flops | bytes accessed | tf_op | source)
XLA Modules:
  0.0 1196.7 jit_solution(8126801174571797452)
XLA Ops:
  10.5 123.0 %all-gather.9.cloned.1.call-done = bf16[2,2,2048,512]{3,2,0,1:T(8,128)(2,1)} async-done(((bf16[2,2,256,512]{3,2,0,1:T(8,128)(2,1)}), bf16[2,2,2048,512]{3,2,0,1:T(8,128)(2,1)}) %all-gather.9.cloned.1.call-update) | async-done | bytes 8388624 | tf_op jit(solution)/shard_map/all_gather | solution.py:64
  149.3 44.6 %reduce-scatter.3.cloned.1.call-done = bf16[2,2,256,512]{3,2,0,1:T(8,128)(2,1)} async-done(((bf16[2,2,256,2048]{3,2,0,1:T(8,128)(2,1)}), bf16[2,2,256,512]{3,2,0,1:T(8,128)(2,1)}) %reduce-scatter.3.cloned.1.call-update) | async-done | bytes 1048592 | tf_op jit(solution)/shard_map/reduce_scatter | solution.py:106
  196.9 34.1 %all-gather.11.cloned.1.call-done = bf16[2,2,256,2048]{3,2,0,1:T(8,128)(2,1)} async-done(((bf16[2,2,256,512]{3,2,0,1:T(8,128)(2,1)}), bf16[2,2,256,2048]{3,2,0,1:T(8,128)(2,1)}) %all-gather.11.cloned.1.call-update) | async-done | bytes 4194320 | tf_op jit(solution)/shard_map/all_gather | solution.py:111
  230.9 17.6 %fusion.45 = f32[2,256,512]{2,1,0:T(8,128)S(1)} fusion(s32[512]{0:T(512)S(1)} %iota_add_fusion, bf16[2,2,256,2048]{3,2,0,1:T(8,128)(2,1)} %all-gather.11.cloned.1.call-done), kind=kOutput, calls=%fused_computation.87 | convolution fusion | flops 1090519040 | bytes 3147776 | tf_op jit(solution)/shard_map/fmn,nc->fmc/dot_general | solution.py:33
  248.5 15.9 %fusion.47 = f32[2,256,512]{2,1,0:T(8,128)S(1)} fusion(s32[512]{0:T(512)S(1)} %iota_add_fusion, bf16[2,2,256,2048]{3,2,0,1:T(8,128)(2,1)S(1)} %copy-done.13), kind=kOutput, calls=%fused_computation.88 | convolution fusion | flops 1090519040 | bytes 3147776 | tf_op jit(solution)/shard_map/fmn,nc->fmc/dot_general | solution.py:33
  264.4 16.4 %fusion.124 = bf16[2,1,256,512]{3,2,0,1:T(8,128)(2,1)S(1)} fusion(f32[2,256,512]{2,1,0:T(8,128)S(1)} %fusion.45, s32[512]{0:T(512)S(1)} %iota_add_fusion, bf16[2,2,256,2048]{3,2,0,1:T(8,128)(2,1)S(1)} %copy-done.13), kind=kOutput, calls=%fused_computation.129 | convolution fusion | flops 1091043328 | bytes 3672064 | tf_op jit(solution)/shard_map/fmn,nc->fmc/dot_general | solution.py:33
  280.8 16.6 %fusion.121 = bf16[2,1,256,512]{3,2,0,1:T(8,128)(2,1)S(1)} fusion(f32[2,256,512]{2,1,0:T(8,128)S(1)} %fusion.47, s32[512]{0:T(512)S(1)} %iota_add_fusion, bf16[2,2,256,2048]{3,2,0,1:T(8,128)(2,1)S(1)} %copy-done.13), kind=kOutput, calls=%fused_computation.128 | convolution fusion | flops 1091043328 | bytes 3672064 | tf_op jit(solution)/shard_map/fmn,nc->fmc/dot_general | solution.py:33
  298.5 122.7 %all-gather.13.cloned.1.call-done = bf16[2,2,2048,512]{3,2,0,1:T(8,128)(2,1)} async-done(((bf16[2,2,256,512]{3,2,0,1:T(8,128)(2,1)}), bf16[2,2,2048,512]{3,2,0,1:T(8,128)(2,1)}) %all-gather.13.cloned.1.call-update) | async-done | bytes 8388624 | tf_op jit(solution)/shard_map/all_gather | solution.py:113
  459.2 41.7 %pmax.14 = f32[2]{0:T(128)S(1)} all-reduce(f32[2]{0:T(128)S(1)} %fusion.160), channel_id=1, replica_groups=mesh['src'=8,'rcv'=4] {'src','rcv'}, use_global_device_ids=true, to_apply=%region_2.3 | all-reduce | flops 2 | bytes 16 | tf_op jit(solution)/shard_map/pmax | solution.py:117
  505.5 122.2 %all-gather.15.cloned.1.call-done = bf16[2,2,2048,512]{2,3,0,1:T(8,128)(2,1)} async-done(((bf16[2,2,256,512]{2,3,0,1:T(8,128)(2,1)}), bf16[2,2,2048,512]{2,3,0,1:T(8,128)(2,1)}) %all-gather.15.cloned.1.call-update) | async-done | bytes 8388624 | tf_op jit(solution)/shard_map/all_gather | solution.py:83
  666.2 34.4 %all-gather.17.cloned.1.call-done = bf16[2,2,256,2048]{2,3,0,1:T(8,128)(2,1)} async-done(((bf16[2,2,256,512]{2,3,0,1:T(8,128)(2,1)}), bf16[2,2,256,2048]{2,3,0,1:T(8,128)(2,1)}) %all-gather.17.cloned.1.call-update) | async-done | bytes 4194320 | tf_op jit(solution)/shard_map/all_gather | solution.py:86
  700.7 18.5 %fusion.41 = f32[2,256,512]{2,1,0:T(8,128)S(1)} fusion(s32[512]{0:T(512)S(1)} %iota_add_fusion, bf16[2,2,256,2048]{2,3,0,1:T(8,128)(2,1)} %all-gather.17.cloned.1.call-done), kind=kOutput, calls=%fused_computation.85 | convolution fusion | flops 1090519040 | bytes 3147776 | tf_op jit(solution)/shard_map/fmn,nc->fmc/dot_general | solution.py:33
  719.1 16.9 %fusion.43 = f32[2,256,512]{2,1,0:T(8,128)S(1)} fusion(s32[512]{0:T(512)S(1)} %iota_add_fusion, bf16[2,2,256,2048]{2,3,0,1:T(8,128)(2,1)S(1)} %copy-done.16), kind=kOutput, calls=%fused_computation.86 | convolution fusion | flops 1090519040 | bytes 3147776 | tf_op jit(solution)/shard_map/fmn,nc->fmc/dot_general | solution.py:33
  736.1 17.2 %fusion.118 = bf16[2,1,256,512]{3,2,0,1:T(8,128)(2,1)S(1)} fusion(f32[2,256,512]{2,1,0:T(8,128)S(1)} %fusion.41, s32[512]{0:T(512)S(1)} %iota_add_fusion, bf16[2,2,256,2048]{2,3,0,1:T(8,128)(2,1)S(1)} %copy-done.16), kind=kOutput, calls=%fused_computation.127 | convolution fusion | flops 1091043328 | bytes 3672064 | tf_op jit(solution)/shard_map/fmn,nc->fmc/dot_general | solution.py:33
  753.3 16.8 %fusion.115 = bf16[2,1,256,512]{3,2,0,1:T(8,128)(2,1)S(1)} fusion(f32[2,256,512]{2,1,0:T(8,128)S(1)} %fusion.43, s32[512]{0:T(512)S(1)} %iota_add_fusion, bf16[2,2,256,2048]{2,3,0,1:T(8,128)(2,1)S(1)} %copy-done.16), kind=kOutput, calls=%fused_computation.126 | convolution fusion | flops 1091043328 | bytes 3672064 | tf_op jit(solution)/shard_map/fmn,nc->fmc/dot_general | solution.py:33
  771.3 34.6 %all-gather.19.cloned.1.call-done = bf16[2,2,256,2048]{3,2,0,1:T(8,128)(2,1)} async-done(((bf16[2,2,256,512]{3,2,0,1:T(8,128)(2,1)}), bf16[2,2,256,2048]{3,2,0,1:T(8,128)(2,1)}) %all-gather.19.cloned.1.call-update) | async-done | bytes 4194320 | tf_op jit(solution)/shard_map/all_gather | solution.py:89
  831.6 44.5 %reduce-scatter.5.cloned.1.call-done = bf16[2,2,256,512]{3,2,0,1:T(8,128)(2,1)} async-done(((bf16[2,2,256,2048]{3,2,0,1:T(8,128)(2,1)}), bf16[2,2,256,512]{3,2,0,1:T(8,128)(2,1)}) %reduce-scatter.5.cloned.1.call-update) | async-done | bytes 1048592 | tf_op jit(solution)/shard_map/reduce_scatter | solution.py:106
  879.1 34.2 %all-gather.21.cloned.1.call-done = bf16[2,2,256,2048]{3,2,0,1:T(8,128)(2,1)} async-done(((bf16[2,2,256,512]{3,2,0,1:T(8,128)(2,1)}), bf16[2,2,256,2048]{3,2,0,1:T(8,128)(2,1)}) %all-gather.21.cloned.1.call-update) | async-done | bytes 4194320 | tf_op jit(solution)/shard_map/all_gather | solution.py:111
  913.2 17.6 %fusion.37 = f32[2,256,512]{2,1,0:T(8,128)S(1)} fusion(s32[512]{0:T(512)S(1)} %iota_add_fusion, bf16[2,2,256,2048]{3,2,0,1:T(8,128)(2,1)} %all-gather.21.cloned.1.call-done), kind=kOutput, calls=%fused_computation.83 | convolution fusion | flops 1090519040 | bytes 3147776 | tf_op jit(solution)/shard_map/fmn,nc->fmc/dot_general | solution.py:33
  946.7 16.4 %fusion.130 = bf16[2,1,256,512]{3,2,0,1:T(8,128)(2,1)S(1)} fusion(f32[2,256,512]{2,1,0:T(8,128)S(1)} %fusion.37, s32[512]{0:T(512)S(1)} %iota_add_fusion, bf16[2,2,256,2048]{3,2,0,1:T(8,128)(2,1)S(1)} %copy-done.15), kind=kOutput, calls=%fused_computation.131 | convolution fusion | flops 1091043328 | bytes 3672064 | tf_op jit(solution)/shard_map/fmn,nc->fmc/dot_general | solution.py:33
  963.1 17.0 %fusion.127 = bf16[2,1,256,512]{3,2,0,1:T(8,128)(2,1)S(1)} fusion(f32[2,256,512]{2,1,0:T(8,128)S(1)} %fusion.39, s32[512]{0:T(512)S(1)} %iota_add_fusion, bf16[2,2,256,2048]{3,2,0,1:T(8,128)(2,1)S(1)} %copy-done.15), kind=kOutput, calls=%fused_computation.130 | convolution fusion | flops 1091043328 | bytes 3672064 | tf_op jit(solution)/shard_map/fmn,nc->fmc/dot_general | solution.py:33
  981.2 45.0 %all-reduce = (f32[2]{0:T(128)S(1)}, f32[2]{0:T(128)S(1)}) all-reduce(f32[2]{0:T(128)S(1)} %get-tuple-element.5, f32[2]{0:T(128)S(1)} %get-tuple-element.4), channel_id=1, replica_groups=mesh['src'=8,'rcv'=4] {'src','rcv'}, use_global_device_ids=true, to_apply=%region_9.10 | all-reduce | flops 4 | bytes 32 | tf_op jit(solution)/shard_map/psum | solution.py:97
  1026.2 78.8 %all-gather.23.cloned.1.call-done = bf16[2,2,2048,512]{3,2,0,1:T(8,128)(2,1)} async-done(((bf16[2,2,256,512]{3,2,0,1:T(8,128)(2,1)}), bf16[2,2,2048,512]{3,2,0,1:T(8,128)(2,1)}) %all-gather.23.cloned.1.call-update) | async-done | bytes 8388624 | tf_op jit(solution)/shard_map/all_gather | solution.py:113
  1143.0 41.7 %pmax.15 = f32[2]{0:T(128)S(1)} all-reduce(f32[2]{0:T(128)S(1)} %fusion.161), channel_id=1, replica_groups=mesh['src'=8,'rcv'=4] {'src','rcv'}, use_global_device_ids=true, to_apply=%region_5.6 | all-reduce | flops 2 | bytes 16 | tf_op jit(solution)/shard_map/pmax | solution.py:117
  (111 shorter events, 193.6 us)
Async XLA Ops:
  7.2 126.4 %all-gather.9.cloned.1.call-start = ((), (), s32[]{:S(2)}) async-start(), calls=%async_computation.2 | async-start | bytes 9437184 | tf_op jit(solution)/shard_map/all_gather | solution.py:64
  9.5 127.9 %copy-start.1 = (bf16[2,2,256,512]{3,2,1,0:T(8,128)(2,1)S(1)}, bf16[2,2,256,512]{3,2,1,0:T(8,128)(2,1)}, u32[]{:S(2)}) copy-start(bf16[2,2,256,512]{3,2,1,0:T(8,128)(2,1)} %param.2) | copy-start | bytes 3145732
  9.5 184.3 %reduce-scatter.3.cloned.1.call-start = ((), (), s32[]{:S(2)}) async-start(), calls=%async_computation.3 | async-start | bytes 5242880 | tf_op jit(solution)/shard_map/reduce_scatter | solution.py:106
  133.5 4.8 copy-start
  149.2 81.7 %all-gather.11.cloned.1.call-start = ((), (), s32[]{:S(2)}) async-start(), calls=%async_computation.4 | async-start | bytes 5242880 | tf_op jit(solution)/shard_map/all_gather | solution.py:111
  196.3 224.9 %all-gather.13.cloned.1.call-start = ((), (), s32[]{:S(2)}) async-start(), calls=%async_computation.5 | async-start | bytes 9437184 | tf_op jit(solution)/shard_map/all_gather | solution.py:113
  230.9 17.6 %copy-start.13 = (bf16[2,2,256,2048]{3,2,0,1:T(8,128)(2,1)S(1)}, bf16[2,2,256,2048]{3,2,0,1:T(8,128)(2,1)}, u32[]{:S(2)}) copy-start(bf16[2,2,256,2048]{3,2,0,1:T(8,128)(2,1)} %all-gather.11.cloned.1.call-done) | copy-start | bytes 12582916
  298.5 329.2 %all-gather.15.cloned.1.call-start = ((), (), s32[]{:S(2)}) async-start(), calls=%async_computation.6 | async-start | bytes 9437184 | tf_op jit(solution)/shard_map/all_gather | solution.py:83
  421.2 10.8 copy-start.10
  449.3 8.4 copy-start.4
  505.3 195.4 %all-gather.17.cloned.1.call-start = ((), (), s32[]{:S(2)}) async-start(), calls=%async_computation.7 | async-start | bytes 5242880 | tf_op jit(solution)/shard_map/all_gather | solution.py:86
  627.7 11.0 copy-start.12
  666.0 139.8 %all-gather.19.cloned.1.call-start = ((), (), s32[]{:S(2)}) async-start(), calls=%async_computation.8 | async-start | bytes 5242880 | tf_op jit(solution)/shard_map/all_gather | solution.py:89
  700.7 18.5 %copy-start.16 = (bf16[2,2,256,2048]{2,3,0,1:T(8,128)(2,1)S(1)}, bf16[2,2,256,2048]{2,3,0,1:T(8,128)(2,1)}, u32[]{:S(2)}) copy-start(bf16[2,2,256,2048]{2,3,0,1:T(8,128)(2,1)} %all-gather.17.cloned.1.call-done) | copy-start | bytes 12582916
  771.2 104.9 %reduce-scatter.5.cloned.1.call-start = ((), (), s32[]{:S(2)}) async-start(), calls=%async_computation.9 | async-start | bytes 5242880 | tf_op jit(solution)/shard_map/reduce_scatter | solution.py:106
  810.0 7.2 slice-start
  831.6 81.7 %all-gather.21.cloned.1.call-start = ((), (), s32[]{:S(2)}) async-start(), calls=%async_computation.10 | async-start | bytes 5242880 | tf_op jit(solution)/shard_map/all_gather | solution.py:111
  878.6 226.4 %all-gather.23.cloned.1.call-start = ((), (), s32[]{:S(2)}) async-start(), calls=%async_computation.11 | async-start | bytes 9437184 | tf_op jit(solution)/shard_map/all_gather | solution.py:113
  913.2 17.6 %copy-start.15 = (bf16[2,2,256,2048]{3,2,0,1:T(8,128)(2,1)S(1)}, bf16[2,2,256,2048]{3,2,0,1:T(8,128)(2,1)}, u32[]{:S(2)}) copy-start(bf16[2,2,256,2048]{3,2,0,1:T(8,128)(2,1)} %all-gather.21.cloned.1.call-done) | copy-start | bytes 12582916
  1105.0 10.8 copy-start.11
  1132.9 8.5 copy-start.8
  1132.9 8.5 copy-start.3
  1132.9 8.5 copy-start.5
  1132.9 8.5 copy-start.7
  (5 other events, 10.8 us)
Sparse Core Ops, SparseCore 0:
  10.7 122.7 all-gather.8
  149.3 44.4 reduce-scatter.2
  196.5 34.4 all-gather.10
  298.6 122.6 all-gather.12
  505.4 122.2 all-gather.14
  666.1 34.4 all-gather.16
  771.3 34.4 all-gather.18
  831.7 44.3 reduce-scatter.4
  878.8 34.4 all-gather.20
  981.3 123.6 all-gather.22
where the time goes:
time: 1200 us
  waiting for transfers between devices  673 us (56%)
  matrix products  345 us (29%)
  blocking collectives  128 us (11%)
  other arithmetic  26.4 us (2%)
  between operations  14.9 us (1%)
    dot_general x28, matrix products, single(): jnp.einsum(pattern, first_op, second_op, preferred_element_type=jnp.float32)  325 us
    all_gather x2, waiting for transfers between devices, per_device(): lax.all_gather(halfway, 'src', axis=2, tiled=True)  202 us
    all_gather x1, waiting for transfers between devices, per_device(): columns_all = lax.all_gather(traces, 'src', axis=2, tiled=True)  123 us
    all_gather x1, waiting for transfers between devices, per_device(): lax.all_gather(coeff_half, 'src', axis=2, tiled=True)  122 us
    reduce_scatter x2, waiting for transfers between devices, per_device(): lax.psum_scatter(scaled.astype(jnp.bfloat16), 'rcv', scatter_dimension=3,...  89.1 us
    pmax x2, blocking collectives, per_device(): global_peak = lax.pmax(local_peak, ('src', 'rcv'))  83.5 us
    all_gather x2, waiting for transfers between devices, per_device(): lax.all_gather(grad_half, 'rcv', axis=3, tiled=True)  68.2 us
    psum x1, blocking collectives, per_device(): norm_list.append(jnp.sqrt(lax.psum(local_squares, ('src', 'rcv'))))  45 us
  transfers between devices with their start and end apart: 10, of which 10 were waited for; matrix products, arithmetic and copies ran while one was open for 0% of the time, Pallas kernels for 0%

commit v1 on v0

v1 whole, which is shorter than its diff:
```python
import functools
import math

import jax
import jax.numpy as jnp
from jax import lax
from jax.experimental import pallas as pl
from jax.experimental.pallas import tpu as pltpu
from jax.sharding import PartitionSpec as P

ITERS = 2
CORES = 2
MESH = pl.DeviceIdType.MESH

step_length = 0.4
shrink_fraction = 0.2


def exchange_kernel(members, whole, x_ref, out_ref, send_sem, recv_sem, own_sem):
    count, me, device = members()
    barrier = pltpu.get_barrier_semaphore()
    for step in range(1, count):
        pl.semaphore_signal(
            barrier, inc=1, device_id=device(lax.rem(me + step, count)), device_id_type=MESH
        )
    pl.semaphore_wait(barrier, count - 1)
    own = pltpu.make_async_copy(x_ref if whole else x_ref.at[me], out_ref.at[me], own_sem)
    own.start()
    sends = []
    for step in range(1, count):
        peer = lax.rem(me + step, count)
        copy = pltpu.make_async_remote_copy(
            src_ref=x_ref if whole else x_ref.at[peer],
            dst_ref=out_ref.at[me],
            send_sem=send_sem.at[step],
            recv_sem=recv_sem.at[step],
            device_id=device(peer),
            device_id_type=MESH,
        )
        copy.start()
        sends.append(copy)
    own.wait()
    for step in range(1, count):
        origin = lax.rem(me - step + count, count)
        pltpu.make_async_remote_copy(
            src_ref=out_ref.at[origin],
            dst_ref=out_ref.at[origin],
            send_sem=send_sem.at[step],
            recv_sem=recv_sem.at[step],
            device_id=device(origin),
            device_id_type=MESH,
        ).wait_recv()
    for copy in sends:
        copy.wait_send()


def exchange(x, members, count, ident, whole=False):
    shape = (count,) + x.shape if whole else x.shape
    return pl.pallas_call(
        functools.partial(exchange_kernel, members, whole),
        out_shape=jax.ShapeDtypeStruct(shape, x.dtype),
        in_specs=[pl.BlockSpec(memory_space=pltpu.VMEM)],
        out_specs=pl.BlockSpec(memory_space=pltpu.VMEM),
        scratch_shapes=[
            pltpu.SemaphoreType.DMA((count,)),
            pltpu.SemaphoreType.DMA((count,)),
            pltpu.SemaphoreType.DMA,
        ],
        compiler_params=pltpu.CompilerParams(collective_id=ident, has_side_effects=True),
    )(x)


def gather_kernel(nz, ny, nf, x_ref, out_ref, own_sem, swap_sem, link_sem, core_sem, send_sem):
    src, rcv = lax.axis_index("src"), lax.axis_index("rcv")
    z, f = src // nf, lax.rem(src, nf)
    y, c = rcv // CORES, lax.rem(rcv, CORES)
    height, width = x_ref.shape[2], x_ref.shape[3]

    def device(zz, ff, yy, cc):
        return (zz * nf + ff, yy * CORES + cc)

    def block(zz, ff, yy, cc):
        top = pl.multiple_of((zz * nf + ff) * height, height)
        left = pl.multiple_of((yy * CORES + cc) * width, width)
        return out_ref.at[:, pl.ds(top, height), pl.ds(left, width)]

    z_peers = [lax.rem(z + d, nz) for d in range(1, nz)]
    y_peers = [lax.rem(y + e, ny) for e in range(1, ny)]
    f_peers = [lax.rem(f + g, nf) for g in range(1, nf)]
    other = 1 - c

    barrier = pltpu.get_barrier_semaphore()
    targets = [device(zz, f, y, c) for zz in z_peers]
    targets += [device(z, f, yy, c) for yy in y_peers]
    targets += [device(z, ff, y, c) for ff in f_peers]
    targets += [device(z, f, y, other)]
    for target in targets:
        pl.semaphore_signal(barrier, inc=1, device_id=target, device_id_type=MESH)
    pl.semaphore_wait(barrier, len(targets))

    sends = []

    def push(source, place, semaphore, target):
        copy = pltpu.make_async_remote_copy(
            src_ref=source,
            dst_ref=place,
            send_sem=send_sem.at[len(sends)],
            recv_sem=semaphore,
            device_id=target,
            device_id_type=MESH,
        )
        copy.start()
        sends.append(copy)

    def await_block(place, semaphore):
        pltpu.make_async_remote_copy(
            src_ref=place,
            dst_ref=place,
            send_sem=send_sem.at[0],
            recv_sem=semaphore,
            device_id=device(z, f, y, other),
            device_id_type=MESH,
        ).wait_recv()

    def across(zz, ff, yy):
        here = block(zz, ff, yy, c)
        push(here, here, core_sem.at[zz, ff, yy], device(z, f, y, other))

    def along_z(ff, yy):
        here = block(z, ff, yy, c)
        for zz in z_peers:
            push(here, here, link_sem.at[z, ff, yy], device(zz, f, y, c))

    def along_y(zz, ff):
        here = block(zz, ff, y, c)
        for yy in y_peers:
            push(here, here, link_sem.at[zz, ff, y], device(z, f, yy, c))

    for step, ff in enumerate(f_peers):
        push(x_ref.at[ff], block(z, f, y, c), swap_sem.at[step], device(z, ff, y, c))
    own = pltpu.make_async_copy(x_ref.at[f], block(z, f, y, c), own_sem)
    own.start()
    own.wait()
    for step in range(nf - 1):
        origin = lax.rem(f - 1 - step + nf, nf)
        await_block(block(z, origin, y, c), swap_sem.at[step])

    for ff in range(nf):
        if ff % 2 == 0:
            along_z(ff, y)
        else:
            along_y(z, ff)
    for ff in range(nf):
        across(z, ff, y)
    for ff in range(nf):
        if ff % 2 == 0:
            along_y(z, ff)
        else:
            along_z(ff, y)
    for ff in range(1, nf, 2):
        for yy in y_peers:
            await_block(block(z, ff, yy, c), link_sem.at[z, ff, yy])
            along_z(ff, yy)
            across(z, ff, yy)
    for ff in range(0, nf, 2):
        for zz in z_peers:
            await_block(block(zz, ff, y, c), link_sem.at[zz, ff, y])
            along_y(zz, ff)
            across(zz, ff, y)
    for ff in range(0, nf, 2):
        for yy in y_peers:
            await_block(block(z, ff, yy, c), link_sem.at[z, ff, yy])
            across(z, ff, yy)
    for ff in range(1, nf, 2):
        for zz in z_peers:
            await_block(block(zz, ff, y, c), link_sem.at[zz, ff, y])
            across(zz, ff, y)
    for ff in range(nf):
        for zz in z_peers:
            for yy in y_peers:
                await_block(block(zz, ff, yy, c), link_sem.at[zz, ff, yy])
                across(zz, ff, yy)
    for ff in range(nf):
        for zz in range(nz):
            for yy in range(ny):
                await_block(block(zz, ff, yy, other), core_sem.at[zz, ff, yy])
    for copy in sends:
        copy.wait_send()


def gather(traces, nz, ny, nf, extent):
    even, odd = (nf + 1) // 2, nf // 2
    total = (nf - 1) + nf * nz * ny
    total += even * ((nz - 1) + nz * (ny - 1)) + odd * ((ny - 1) + ny * (nz - 1))
    return pl.pallas_call(
        functools.partial(gather_kernel, nz, ny, nf),
        out_shape=jax.ShapeDtypeStruct((2, extent, extent), traces.dtype),
        in_specs=[pl.BlockSpec(memory_space=pltpu.VMEM)],
        out_specs=pl.BlockSpec(memory_space=pl.ANY),
        scratch_shapes=[
            pltpu.SemaphoreType.DMA,
            pltpu.SemaphoreType.DMA((nf,)),
            pltpu.SemaphoreType.DMA((nz, nf, ny)),
            pltpu.SemaphoreType.DMA((nz, nf, ny)),
            pltpu.SemaphoreType.DMA((total + nf * (nz + ny),)),
        ],
        compiler_params=pltpu.CompilerParams(collective_id=0, has_side_effects=True),
    )(traces)


def tables(extent):
    low = 1 << (extent.bit_length() // 2)
    while extent % low:
        low //= 2
    row = jnp.arange(extent, dtype=jnp.int32)

    def parts(column, scale):
        phase = row[:, None] * column[None, :] % extent
        angle = phase.astype(jnp.float32) * (2.0 * math.pi / extent)
        return lax.optimization_barrier((jnp.cos(angle) * scale, jnp.sin(angle) * scale))

    cos_low, sin_low = parts(jnp.arange(low, dtype=jnp.int32), 1.0)
    cos_high, sin_high = parts(
        jnp.arange(extent // low, dtype=jnp.int32) * low, 1.0 / math.sqrt(extent)
    )
    cos_high, sin_high = jnp.repeat(cos_high, low, 1), jnp.repeat(sin_high, low, 1)
    cos_low = jnp.tile(cos_low, (1, extent // low))
    sin_low = jnp.tile(sin_low, (1, extent // low))
    cosine = (cos_high * cos_low - sin_high * sin_low).astype(jnp.bfloat16)
    sine = (sin_high * cos_low + cos_high * sin_low).astype(jnp.bfloat16)
    return lax.optimization_barrier((cosine, sine))


def dot(left, right, pattern="mn,nc->mc"):
    return jnp.einsum(pattern, left, right, preferred_element_type=jnp.float32)


def per_device(nsrc, nrcv, traces, wavelet):
    nf, extent = traces.shape[0], traces.shape[2] * nsrc
    nz, ny = nsrc // nf, nrcv // CORES
    group = nz * nrcv
    part = extent // group
    src, rcv = lax.axis_index("src"), lax.axis_index("rcv")
    f = lax.rem(src, nf)
    place = rcv * nz + src // nf

    def same_frequency():
        src, rcv = lax.axis_index("src"), lax.axis_index("rcv")
        f = lax.rem(src, nf)
        return group, rcv * nz + src // nf, lambda i: (lax.rem(i, nz) * nf + f, i // nz)

    def same_column():
        rcv = lax.axis_index("rcv")
        return nsrc, lax.axis_index("src"), lambda i: (i, rcv)

    def everyone():
        me = lax.axis_index("src") * nrcv + lax.axis_index("rcv")
        return nsrc * nrcv, me, lambda i: (i // nrcv, lax.rem(i, nrcv))

    root_scale = 1.0 / math.sqrt(extent)
    wave = lax.dynamic_slice_in_dim(wavelet, f, 1, 0)[0] * root_scale
    wave_re, wave_im = wave[0], wave[1]

    cosine, sine = tables(extent)
    data = gather(traces, nz, ny, nf, extent)
    data_re, data_im = data[0], data[1]
    rows = lax.dynamic_slice_in_dim(data, place * part, part, 1)

    def rows_times(left, first, second, pattern="mn,nc->mc"):
        stacked = left.reshape(2 * part, extent)
        a = dot(stacked, first, pattern).reshape(2, part, extent)
        b = dot(stacked, second, pattern).reshape(2, part, extent)
        return a[0], a[1], b[0], b[1]

    def times_columns(right):
        a = dot(cosine, right).reshape(extent, 2, part)
        b = dot(sine, right).reshape(extent, 2, part)
        return a[:, 0], a[:, 1], b[:, 0], b[:, 1]

    coeffs_re = jnp.zeros((extent, part), jnp.float32)
    coeffs_im = coeffs_re
    norm_list = []
    for iteration in range(ITERS):
        if iteration == 0:
            misfit = rows.astype(jnp.float32)
        else:
            stacked = jnp.concatenate([coeffs_re, coeffs_im], 1).astype(jnp.bfloat16)
            re_c, im_c, re_s, im_s = times_columns(stacked)
            halfway = jnp.concatenate([re_c - im_s, im_c + re_s], 1).astype(jnp.bfloat16)
            halfway = exchange(halfway.reshape(group, part, 2 * part), same_frequency, group, 1)
            halfway = halfway.reshape(group, part, 2, part).transpose(2, 1, 0, 3)
            re_c, im_c, re_s, im_s = rows_times(halfway.reshape(2, part, extent), cosine, sine)
            model = jnp.stack([re_c - im_s, re_s + im_c]).astype(jnp.bfloat16)
            re_r, im_r, re_i, im_i = rows_times(model, data_re, data_im)
            prod_re, prod_im = re_r - im_i, re_i + im_r
            misfit = (
                rows.astype(jnp.float32)
                - model.astype(jnp.float32)
                + jnp.stack(
                    [
                        prod_re * wave_re - prod_im * wave_im,
                        prod_re * wave_im + prod_im * wave_re,
                    ]
                )
            )
        squares = jnp.sum(misfit * misfit)
        misfit_half = misfit.astype(jnp.bfloat16)
        re_r, im_r, re_i, im_i = rows_times(misfit_half, data_re, data_im, "mr,kr->mk")
        back_re, back_im = re_r + im_i, im_r - re_i
        scaled = jnp.stack(
            [back_re * wave_re + back_im * wave_im, back_im * wave_re - back_re * wave_im]
        )
        grad_half = (misfit_half.astype(jnp.float32) - scaled).astype(jnp.bfloat16)
        re_c, im_c, re_s, im_s = rows_times(grad_half, cosine, sine)
        turned = jnp.stack([re_c + im_s, im_c - re_s]).astype(jnp.bfloat16)
        turned = turned.reshape(2, part, group, part).transpose(2, 0, 1, 3)
        turned = exchange(turned, same_frequency, group, 2)
        turned = turned.transpose(0, 2, 1, 3).reshape(extent, 2 * part)
        re_c, im_c, re_s, im_s = times_columns(turned)
        trial_re = coeffs_re + step_length * (re_c + im_s)
        trial_im = coeffs_im + step_length * (im_c - re_s)
        magnitude = jnp.sqrt(trial_re * trial_re + trial_im * trial_im)
        upper = lax.broadcasted_iota(jnp.int32, (8, 128), 0) < 4
        tile = jnp.where(upper, jnp.max(magnitude), squares)
        gathered = exchange(tile, everyone, nsrc * nrcv, 3, whole=True)
        gathered = gathered.reshape(nz, nf, nrcv, 8, 128)
        norm_list.append(jnp.sqrt(jnp.sum(gathered[:, :, :, 4, 0], axis=(0, 2))))
        peaks = jnp.max(gathered[:, :, :, 0, 0], axis=(0, 2))
        level = shrink_fraction * lax.dynamic_slice_in_dim(peaks, f, 1, 0)[0]
        factor = jnp.maximum(1.0 - level / jnp.maximum(magnitude, level), 0.0)
        coeffs_re, coeffs_im = trial_re * factor, trial_im * factor
    stacked = jnp.concatenate([coeffs_re, coeffs_im], 1).astype(jnp.bfloat16)
    spread = exchange(stacked.reshape(nsrc, extent // nsrc, 2 * part), same_column, nsrc, 4)
    spread = spread.reshape(nz, nf, extent // nsrc, 2, part).transpose(1, 3, 2, 0, 4)
    coeffs = spread.reshape(traces.shape).astype(jnp.float32)
    return (coeffs, jnp.stack(norm_list))


def solution(mesh):
    in_specs = (P(None, None, "src", "rcv"), P())
    out_specs = (P(None, None, "src", "rcv"), P())
    body = functools.partial(per_device, mesh.shape["src"], mesh.shape["rcv"])
    return jax.shard_map(body, mesh=mesh, in_specs=in_specs, out_specs=out_specs, check_vma=False)
```

time: 1200 us -> 462 us (0.39)
  waiting for transfers between devices: 673 us -> 0 us
  Pallas kernels: 0 us -> 294 us
  matrix products: 345 us -> 76.6 us
  blocking collectives: 128 us -> 0 us
  local copies, waits for them, and re-layouts: 7.09 us -> 38.7 us
  other arithmetic: 26.4 us -> 45.2 us
  between operations: 14.9 us -> 2.87 us
    all_gather x8 -> x0, waiting for transfers between devices: 584 us -> none  [the longest x2 202 us: per_device(): lax.all_gather(halfway, 'src', axis=2, tiled=True)]
    pallas_call x0 -> x7, Pallas kernels: none -> 294 us  [the longest x1 156 us: gather(): pl.pallas_call(functools.partial(gather_kernel, nz, ny, nf), out_shape=ja...]
    dot_general x36 -> x18, matrix products: 345 us -> 76.6 us  [dot(): return jnp.einsum(pattern, left, right, preferred_element_type=jnp.float32)]
    reduce_scatter x2 -> x0, waiting for transfers between devices: 89.1 us -> none  [per_device(): lax.psum_scatter(scaled.astype(jnp.bfloat16), 'rcv', scatter_dimension=3,...]
    pmax x2 -> x0, blocking collectives: 83.5 us -> none  [per_device(): global_peak = lax.pmax(local_peak, ('src', 'rcv'))]
    psum x1 -> x0, blocking collectives: 45 us -> none  [per_device(): norm_list.append(jnp.sqrt(lax.psum(local_squares, ('src', 'rcv'))))]
  transfers between devices with their start and end apart: 10 -> 0, of which waited for: 10 -> 0; matrix products, arithmetic and copies ran while one was open for 0% -> 0% of each run, Pallas kernels for 0% -> 0%
where the time goes in v1:
time: 462 us; the launch traced here: 457 us
  Pallas kernels  294 us (64%)
  matrix products  76.6 us (17%)
  other arithmetic  45.2 us (10%)
  local copies, waits for them, and re-layouts  38.7 us (8%)
    pallas_call x1, Pallas kernels, gather(): pl.pallas_call(functools.partial(gather_kernel, nz, ny, nf), out_shape=ja...  156 us
    pallas_call x6, Pallas kernels, exchange(): pl.pallas_call(functools.partial(exchange_kernel, members, whole), out_sh...  138 us
    dot_general x18, matrix products, dot(): return jnp.einsum(pattern, left, right, preferred_element_type=jnp.float32)  76.6 us
    unnamed x34, local copies, waits for them, and re-layouts  11.5 us

profile of v1, /device:TPU:14, one launch (start us, length us, event | category | flops | bytes accessed | tf_op | source)
XLA Modules:
  0.0 457.1 jit_solution(10202902508213424871)
XLA Ops:
  5.1 8.3 %add_convert_fusion = (bf16[2048,32,64]{0,2,1:T(8,128)(2,1)}, bf16[2048,32,64]{0,2,1:T(8,128)(2,1)}) fusion(f32[2048,64]{0,1:T(8,128)S(1)} %get-tuple-element.11, f32[2048,32]{0,1:T(8,128)S(1)} %get-tuple-element.10, f32[2048,64]{0,1:T(8,128)S(1)} %get-tuple-element.9, f32[2048,32]{0,1:T(8,128)S(1)} %get-tuple-element.8), kind=kLoop, calls=%fused_computation | loop fusion | flops 33554432 | bytes 18350080 | tf_op jit(solution)/shard_map/convert_element_type | solution.py:230
  13.5 155.8 %shard_map.41 = bf16[2,2048,2048]{2,1,0:T(8,128)(2,1)} custom-call(bf16[2,2,256,512]{3,2,1,0:T(8,128)(2,1)} %x_ref.1), custom_call_target="tpu_custom_call" | custom-call | tf_op jit(solution)/shard_map/pallas_call | solution.py:195
  171.9 6.4 %fusion.8 = f32[256,2048]{1,0:T(8,128)S(1)} fusion(bf16[256,2048]{1,0:T(8,128)(2,1)S(1)} %bitcast.188, bf16[2,2048,2048]{2,1,0:T(8,128)(2,1)} %shard_map.41), kind=kOutput, calls=%fused_computation.10 | convolution fusion | flops 2147483648 | bytes 11534336 | tf_op jit(solution)/shard_map/mr,kr->mk/dot_general | solution.py:235
  182.8 5.9 %fusion.85 = f32[256,2048]{1,0:T(8,128)S(1)} fusion(bf16[256,2048]{1,0:T(8,128)(2,1)S(1)} %bitcast.235, bf16[2048,2048]{0,1:T(8,128)(2,1)} %bitcast.202), kind=kOutput, calls=%fused_computation.153 | convolution fusion | flops 2147483648 | bytes 11534336 | tf_op jit(solution)/shard_map/mn,nc->mc/dot_general | solution.py:235
  193.6 28.2 %shard_map.42 = bf16[16,2,128,128]{3,2,1,0:T(8,128)(2,1)} custom-call(bf16[16,2,128,128]{3,2,1,0:T(8,128)(2,1)} %maximum_bitcast_fusion.x_ref), custom_call_target="tpu_custom_call" | custom-call | tf_op jit(solution)/shard_map/pallas_call | solution.py:59
  224.5 5.0 %fusion.2 = f32[2048,2,128]{2,0,1:T(8,128)S(1)} fusion(bf16[2,128,2048]{2,1,0:T(8,128)(2,1)S(1)} %bitcast.227, bf16[2048,2048]{0,1:T(8,128)(2,1)} %bitcast.203), kind=kOutput, calls=%fused_computation.4 | convolution fusion | flops 2147483648 | bytes 11534336 | tf_op jit(solution)/shard_map/mn,nc->mc/dot_general | solution.py:235
  230.2 2.7 fusion.18
  235.8 10.8 %shard_map.43 = f32[32,8,128]{2,1,0:T(8,128)} custom-call(f32[8,128]{1,0:T(8,128)} %iota.30.x_ref), custom_call_target="tpu_custom_call" | custom-call | tf_op jit(solution)/shard_map/pallas_call | solution.py:59
  249.7 6.1 %fusion.53 = f32[2048,256]{0,1:T(8,128)S(1)} fusion(bf16[2048,2048]{0,1:T(8,128)(2,1)} %bitcast.204, bf16[2048,128]{1,0:T(8,128)(2,1)S(1)} %get-tuple-element.48, bf16[2048,128]{1,0:T(8,128)(2,1)S(1)} %get-tuple-element.47), kind=kOutput, calls=%fused_computation.108 | convolution fusion | flops 2149580800 | bytes 11534336 | tf_op jit(solution)/shard_map/mn,nc->mc/dot_general | solution.py:235
  262.6 6.0 %fusion.54 = f32[2048,256]{0,1:T(8,128)S(1)} fusion(bf16[2048,2048]{0,1:T(8,128)(2,1)} %bitcast.190, bf16[2048,128]{1,0:T(8,128)(2,1)} %copy-done.3, bf16[2048,128]{1,0:T(8,128)(2,1)} %copy-done.2), kind=kOutput, calls=%fused_computation.109 | convolution fusion | flops 2149580800 | bytes 11534336 | tf_op jit(solution)/shard_map/mn,nc->mc/dot_general | solution.py:235
  270.1 2.6 copy.37
  280.5 29.1 %shard_map.44 = bf16[16,128,256]{2,1,0:T(8,128)(2,1)} custom-call(bf16[16,128,256]{2,1,0:T(8,128)(2,1)} %pad_maximum_fusion.1.x_ref), custom_call_target="tpu_custom_call" | custom-call | tf_op jit(solution)/shard_map/pallas_call | solution.py:59
  313.8 5.9 %fusion.30 = f32[256,2048]{1,0:T(8,128)S(1)} fusion(bf16[2048,2048]{0,1:T(8,128)(2,1)} %bitcast.205, bf16[32,8,16,128]{3,2,1,0:T(8,128)(2,1)S(1)} %bitcast.229), kind=kOutput, calls=%fused_computation.38 | convolution fusion | flops 2147483648 | bytes 11534336 | tf_op jit(solution)/shard_map/mn,nc->mc/dot_general | solution.py:235
  319.7 5.9 %fusion.32 = f32[256,2048]{1,0:T(8,128)S(1)} fusion(bf16[2048,2048]{0,1:T(8,128)(2,1)} %bitcast.191, bf16[32,8,16,128]{3,2,1,0:T(8,128)(2,1)S(1)} %bitcast.230), kind=kOutput, calls=%fused_computation.40 | convolution fusion | flops 2147483648 | bytes 11534336 | tf_op jit(solution)/shard_map/mn,nc->mc/dot_general | solution.py:235
  336.2 2.6 fusion.10
  340.9 5.9 %fusion.87 = f32[256,2048]{1,0:T(8,128)S(1)} fusion(bf16[256,2048]{1,0:T(8,128)(2,1)S(1)} %bitcast.233, bf16[2048,2048]{0,1:T(8,128)(2,1)} %bitcast.206), kind=kOutput, calls=%fused_computation.155 | convolution fusion | flops 2147483648 | bytes 11534336 | tf_op jit(solution)/shard_map/mn,nc->mc/dot_general | solution.py:235
  355.3 29.3 %shard_map.45 = bf16[16,2,128,128]{3,2,1,0:T(8,128)(2,1)} custom-call(bf16[16,2,128,128]{3,2,1,0:T(8,128)(2,1)} %maximum_bitcast_fusion.1.x_ref), custom_call_target="tpu_custom_call" | custom-call | tf_op jit(solution)/shard_map/pallas_call | solution.py:59
  386.8 4.9 %fusion = f32[2048,2,128]{2,0,1:T(8,128)S(1)} fusion(bf16[2,128,2048]{2,1,0:T(8,128)(2,1)S(1)} %bitcast.225, bf16[2048,2048]{0,1:T(8,128)(2,1)} %bitcast.207), kind=kOutput, calls=%fused_computation.2 | convolution fusion | flops 2147483648 | bytes 11534336 | tf_op jit(solution)/shard_map/mn,nc->mc/dot_general | solution.py:235
  391.7 5.1 %fusion.16 = f32[2048,2,128]{2,0,1:T(8,128)S(1)} fusion(bf16[2,128,2048]{2,1,0:T(8,128)(2,1)S(1)} %bitcast.226, bf16[2048,2048]{0,1:T(8,128)(2,1)} %bitcast.192), kind=kOutput, calls=%fused_computation.18 | convolution fusion | flops 2147483648 | bytes 11534336 | tf_op jit(solution)/shard_map/mn,nc->mc/dot_general | solution.py:235
  396.8 2.7 fusion.47
  401.4 10.7 %shard_map.46 = f32[32,8,128]{2,1,0:T(8,128)} custom-call(f32[8,128]{1,0:T(8,128)} %iota.31.x_ref), custom_call_target="tpu_custom_call" | custom-call | tf_op jit(solution)/shard_map/pallas_call | solution.py:59
  419.3 29.7 %shard_map.47 = bf16[8,256,256]{2,1,0:T(8,128)(2,1)} custom-call(bf16[8,256,256]{2,1,0:T(8,128)(2,1)} %pad_maximum_fusion.3.x_ref), custom_call_target="tpu_custom_call" | custom-call | tf_op jit(solution)/shard_map/pallas_call | solution.py:59
  451.1 2.7 copy.28
  453.8 3.0 reshape.319
  (95 shorter events, 78.7 us)
Async XLA Ops:
  169.3 9.0 %copy-start = (bf16[2,2048,2048]{2,1,0:T(8,128)(2,1)S(1)}, bf16[2,2048,2048]{2,1,0:T(8,128)(2,1)}, u32[]{:S(2)}) copy-start(bf16[2,2048,2048]{2,1,0:T(8,128)(2,1)} %shard_map.41) | copy-start | bytes 50331652
  182.4 6.2 %slice-start.4 = ((s8[8388608]{0:T(1024)(128)(4,1)}), s8[4194304]{0:T(1024)(128)(4,1)S(1)}, s32[]{:S(2)}) async-start(s8[8388608]{0:T(1024)(128)(4,1)} %bitcast.193), calls=%async_computation.4 | async-start | bytes 8388608
  182.7 5.9 %slice-start.5 = ((s8[8388608]{0:T(1024)(128)(4,1)}), s8[4194304]{0:T(1024)(128)(4,1)S(1)}, s32[]{:S(2)}) async-start(s8[8388608]{0:T(1024)(128)(4,1)} %bitcast.193), calls=%async_computation.5 | async-start | bytes 8388608
  224.2 5.3 %slice-start.6 = ((s8[8388608]{0:T(1024)(128)(4,1)}), s8[4194304]{0:T(1024)(128)(4,1)S(1)}, s32[]{:S(2)}) async-start(s8[8388608]{0:T(1024)(128)(4,1)} %bitcast.196), calls=%async_computation.6 | async-start | bytes 8388608
  224.5 5.7 %slice-start.7 = ((s8[8388608]{0:T(1024)(128)(4,1)}), s8[4194304]{0:T(1024)(128)(4,1)S(1)}, s32[]{:S(2)}) async-start(s8[8388608]{0:T(1024)(128)(4,1)} %bitcast.196), calls=%async_computation.7 | async-start | bytes 8388608
  249.7 6.2 %copy-start.2 = (bf16[2048,128]{1,0:T(8,128)(2,1)}, bf16[2048,128]{1,0:T(8,128)(2,1)S(1)}, u32[]{:S(2)}) copy-start(bf16[2048,128]{1,0:T(8,128)(2,1)S(1)} %get-tuple-element.47) | copy-start | bytes 1572868
  249.7 6.2 %copy-start.3 = (bf16[2048,128]{1,0:T(8,128)(2,1)}, bf16[2048,128]{1,0:T(8,128)(2,1)S(1)}, u32[]{:S(2)}) copy-start(bf16[2048,128]{1,0:T(8,128)(2,1)S(1)} %get-tuple-element.48) | copy-start | bytes 1572868
  277.6 1.7 copy-start.1
  313.8 12.4 %slice-start = ((s8[16777216]{0:T(1024)(128)(4,1)}), s8[4194304]{0:T(1024)(128)(4,1)S(1)}, s32[]{:S(2)}) async-start(s8[16777216]{0:T(1024)(128)(4,1)} %bitcast.184), calls=%async_computation | async-start | bytes 8388608
  313.8 12.4 %slice-start.1 = ((s8[16777216]{0:T(1024)(128)(4,1)}), s8[4194304]{0:T(1024)(128)(4,1)S(1)}, s32[]{:S(2)}) async-start(s8[16777216]{0:T(1024)(128)(4,1)} %bitcast.184), calls=%async_computation.1 | async-start | bytes 8388608
  319.7 6.5 %slice-start.2 = ((s8[16777216]{0:T(1024)(128)(4,1)}), s8[4194304]{0:T(1024)(128)(4,1)S(1)}, s32[]{:S(2)}) async-start(s8[16777216]{0:T(1024)(128)(4,1)} %bitcast.184), calls=%async_computation.2 | async-start | bytes 8388608
  319.7 6.5 %slice-start.3 = ((s8[16777216]{0:T(1024)(128)(4,1)}), s8[4194304]{0:T(1024)(128)(4,1)S(1)}, s32[]{:S(2)}) async-start(s8[16777216]{0:T(1024)(128)(4,1)} %bitcast.184), calls=%async_computation.3 | async-start | bytes 8388608
  340.6 6.2 %slice-start.8 = ((s8[8388608]{0:T(1024)(128)(4,1)}), s8[4194304]{0:T(1024)(128)(4,1)S(1)}, s32[]{:S(2)}) async-start(s8[8388608]{0:T(1024)(128)(4,1)} %bitcast.199), calls=%async_computation.8 | async-start | bytes 8388608
  340.9 5.9 %slice-start.9 = ((s8[8388608]{0:T(1024)(128)(4,1)}), s8[4194304]{0:T(1024)(128)(4,1)S(1)}, s32[]{:S(2)}) async-start(s8[8388608]{0:T(1024)(128)(4,1)} %bitcast.199), calls=%async_computation.9 | async-start | bytes 8388608

commit v2 on v1

--- a/solution.py
+++ b/solution.py
@@ -273,9 +273,8 @@
         return a[0], a[1], b[0], b[1]
 
     def times_columns(right):
-        a = dot(cosine, right).reshape(extent, 2, part)
-        b = dot(sine, right).reshape(extent, 2, part)
-        return a[:, 0], a[:, 1], b[:, 0], b[:, 1]
+        a, b = dot(cosine, right), dot(sine, right)
+        return a[:, :part], a[:, part:], b[:, :part], b[:, part:]
 
     coeffs_re = jnp.zeros((extent, part), jnp.float32)
     coeffs_im = coeffs_re

time: 462 us -> 444 us (0.961)
  local copies, waits for them, and re-layouts: 38.7 us -> 21.7 us
    unnamed x34, local copies, waits for them, and re-layouts: 11.5 us -> 1 us
where the time goes in v2:
time: 444 us; the launch traced here: 439 us
  Pallas kernels  294 us (66%)
  matrix products  78.9 us (18%)
  other arithmetic  41.9 us (9%)
  local copies, waits for them, and re-layouts  21.7 us (5%)
    pallas_call x1, Pallas kernels, gather(): pl.pallas_call(functools.partial(gather_kernel, nz, ny, nf), out_shape=ja...  156 us
    pallas_call x6, Pallas kernels, exchange(): pl.pallas_call(functools.partial(exchange_kernel, members, whole), out_sh...  138 us
    dot_general x18, matrix products, dot(): return jnp.einsum(pattern, left, right, preferred_element_type=jnp.float32)  78.9 us

profile of v2, /device:TPU:14, one launch (start us, length us, event | category | flops | bytes accessed | tf_op | source)
XLA Modules:
  0.0 439.2 jit_solution(551162471305439992)
XLA Ops:
  5.1 8.5 %add_convert_fusion = (bf16[2048,32,64]{0,2,1:T(8,128)(2,1)}, bf16[2048,32,64]{0,2,1:T(8,128)(2,1)}) fusion(f32[2048,64]{0,1:T(8,128)S(1)} %get-tuple-element.11, f32[2048,32]{0,1:T(8,128)S(1)} %get-tuple-element.10, f32[2048,64]{0,1:T(8,128)S(1)} %get-tuple-element.9, f32[2048,32]{0,1:T(8,128)S(1)} %get-tuple-element.8), kind=kLoop, calls=%fused_computation | loop fusion | flops 33554432 | bytes 18350080 | tf_op jit(solution)/shard_map/convert_element_type | solution.py:230
  13.7 155.8 %shard_map.41 = bf16[2,2048,2048]{2,1,0:T(8,128)(2,1)} custom-call(bf16[2,2,256,512]{3,2,1,0:T(8,128)(2,1)} %x_ref.1), custom_call_target="tpu_custom_call" | custom-call | tf_op jit(solution)/shard_map/pallas_call | solution.py:195
  172.1 6.4 %fusion.4 = f32[256,2048]{1,0:T(8,128)S(1)} fusion(bf16[256,2048]{1,0:T(8,128)(2,1)S(1)} %bitcast.112, bf16[2,2048,2048]{2,1,0:T(8,128)(2,1)} %shard_map.41), kind=kOutput, calls=%fused_computation.6 | convolution fusion | flops 2147483648 | bytes 11534336 | tf_op jit(solution)/shard_map/mr,kr->mk/dot_general | solution.py:235
  182.9 5.9 %fusion.87 = f32[256,2048]{1,0:T(8,128)S(1)} fusion(bf16[256,2048]{1,0:T(8,128)(2,1)S(1)} %bitcast.157, bf16[2048,2048]{0,1:T(8,128)(2,1)} %bitcast.126), kind=kOutput, calls=%fused_computation.146 | convolution fusion | flops 2147483648 | bytes 11534336 | tf_op jit(solution)/shard_map/mn,nc->mc/dot_general | solution.py:235
  193.8 28.2 %shard_map.42 = bf16[16,2,128,128]{3,2,1,0:T(8,128)(2,1)} custom-call(bf16[16,2,128,128]{3,2,1,0:T(8,128)(2,1)} %maximum_bitcast_fusion.x_ref), custom_call_target="tpu_custom_call" | custom-call | tf_op jit(solution)/shard_map/pallas_call | solution.py:59
  222.0 3.1 copy.9
  225.1 6.2 %fusion.30 = f32[2048,256]{1,0:T(8,128)S(1)} fusion(bf16[2048,2048]{0,1:T(8,128)(2,1)} %bitcast.127, bf16[32,8,16,128]{3,2,1,0:T(8,128)(2,1)} %bitcast.149), kind=kOutput, calls=%fused_computation.37 | convolution fusion | flops 2147483648 | bytes 11534336 | tf_op jit(solution)/shard_map/mn,nc->mc/dot_general | solution.py:235
  231.3 6.1 %fusion.32 = f32[2048,256]{1,0:T(8,128)S(1)} fusion(bf16[2048,2048]{0,1:T(8,128)(2,1)} %bitcast.114, bf16[32,8,16,128]{3,2,1,0:T(8,128)(2,1)S(1)} %bitcast.150), kind=kOutput, calls=%fused_computation.39 | convolution fusion | flops 2147483648 | bytes 11534336 | tf_op jit(solution)/shard_map/mn,nc->mc/dot_general | solution.py:235
  240.6 10.8 %shard_map.43 = f32[32,8,128]{2,1,0:T(8,128)} custom-call(f32[8,128]{1,0:T(8,128)} %iota.30.x_ref), custom_call_target="tpu_custom_call" | custom-call | tf_op jit(solution)/shard_map/pallas_call | solution.py:59
  253.8 3.8 fusion.83
  257.6 6.2 %fusion.54 = f32[2048,256]{1,0:T(8,128)S(1)} fusion(bf16[2048,2048]{0,1:T(8,128)(2,1)} %bitcast.128, bf16[2048,128]{1,0:T(8,128)(2,1)S(1)} %get-tuple-element.23, bf16[2048,128]{1,0:T(8,128)(2,1)S(1)} %get-tuple-element.39), kind=kOutput, calls=%fused_computation.100 | convolution fusion | flops 2149580800 | bytes 11534336 | tf_op jit(solution)/shard_map/mn,nc->mc/dot_general | solution.py:235
  267.7 29.1 %shard_map.44 = bf16[16,128,256]{2,1,0:T(8,128)(2,1)} custom-call(bf16[16,128,256]{2,1,0:T(8,128)(2,1)} %pad_maximum_fusion.1.x_ref), custom_call_target="tpu_custom_call" | custom-call | tf_op jit(solution)/shard_map/pallas_call | solution.py:59
  299.1 5.9 %fusion.26 = f32[256,2048]{1,0:T(8,128)S(1)} fusion(bf16[2048,2048]{0,1:T(8,128)(2,1)} %bitcast.129, bf16[32,8,16,128]{3,2,1,0:T(8,128)(2,1)S(1)} %bitcast.151), kind=kOutput, calls=%fused_computation.33 | convolution fusion | flops 2147483648 | bytes 11534336 | tf_op jit(solution)/shard_map/mn,nc->mc/dot_general | solution.py:235
  305.0 5.9 %fusion.28 = f32[256,2048]{1,0:T(8,128)S(1)} fusion(bf16[2048,2048]{0,1:T(8,128)(2,1)} %bitcast.115, bf16[32,8,16,128]{3,2,1,0:T(8,128)(2,1)S(1)} %bitcast.152), kind=kOutput, calls=%fused_computation.35 | convolution fusion | flops 2147483648 | bytes 11534336 | tf_op jit(solution)/shard_map/mn,nc->mc/dot_general | solution.py:235
  319.0 3.7 fusion
  322.7 3.9 fusion.6
  326.6 3.9 add_bitcast_fusion
  339.1 29.3 %shard_map.45 = bf16[16,2,128,128]{3,2,1,0:T(8,128)(2,1)} custom-call(bf16[16,2,128,128]{3,2,1,0:T(8,128)(2,1)} %maximum_bitcast_fusion.1.x_ref), custom_call_target="tpu_custom_call" | custom-call | tf_op jit(solution)/shard_map/pallas_call | solution.py:59
  370.6 5.9 %fusion.22 = f32[2048,256]{1,0:T(8,128)S(1)} fusion(bf16[2048,2048]{0,1:T(8,128)(2,1)} %bitcast.130, bf16[32,8,16,128]{3,2,1,0:T(8,128)(2,1)S(1)} %bitcast.147), kind=kOutput, calls=%fused_computation.29 | convolution fusion | flops 2147483648 | bytes 11534336 | tf_op jit(solution)/shard_map/mn,nc->mc/dot_general | solution.py:235
  376.5 6.0 %fusion.24 = f32[2048,256]{1,0:T(8,128)S(1)} fusion(bf16[2048,2048]{0,1:T(8,128)(2,1)} %bitcast.116, bf16[32,8,16,128]{3,2,1,0:T(8,128)(2,1)S(1)} %bitcast.148), kind=kOutput, calls=%fused_computation.31 | convolution fusion | flops 2147483648 | bytes 11534336 | tf_op jit(solution)/shard_map/mn,nc->mc/dot_general | solution.py:235
  385.7 10.8 %shard_map.46 = f32[32,8,128]{2,1,0:T(8,128)} custom-call(f32[8,128]{1,0:T(8,128)} %iota.31.x_ref), custom_call_target="tpu_custom_call" | custom-call | tf_op jit(solution)/shard_map/pallas_call | solution.py:59
  401.2 29.7 %shard_map.47 = bf16[8,256,256]{2,1,0:T(8,128)(2,1)} custom-call(bf16[8,256,256]{2,1,0:T(8,128)(2,1)} %pad_maximum_fusion.3.x_ref), custom_call_target="tpu_custom_call" | custom-call | tf_op jit(solution)/shard_map/pallas_call | solution.py:59
  433.0 2.7 copy.16
  435.7 3.0 reshape.259
  (92 shorter events, 55.2 us)
Async XLA Ops:
  169.5 9.0 %copy-start = (bf16[2,2048,2048]{2,1,0:T(8,128)(2,1)S(1)}, bf16[2,2048,2048]{2,1,0:T(8,128)(2,1)}, u32[]{:S(2)}) copy-start(bf16[2,2048,2048]{2,1,0:T(8,128)(2,1)} %shard_map.41) | copy-start | bytes 50331652
  182.5 6.3 %slice-start.4 = ((s8[8388608]{0:T(1024)(128)(4,1)}), s8[4194304]{0:T(1024)(128)(4,1)S(1)}, s32[]{:S(2)}) async-start(s8[8388608]{0:T(1024)(128)(4,1)} %bitcast.117), calls=%async_computation.4 | async-start | bytes 8388608
  182.9 5.9 %slice-start.5 = ((s8[8388608]{0:T(1024)(128)(4,1)}), s8[4194304]{0:T(1024)(128)(4,1)S(1)}, s32[]{:S(2)}) async-start(s8[8388608]{0:T(1024)(128)(4,1)} %bitcast.117), calls=%async_computation.5 | async-start | bytes 8388608
  225.1 6.2 %copy-start.4 = (bf16[16,128,2,128]{1,0,3,2:T(8,128)(2,1)S(1)}, bf16[16,128,2,128]{1,0,3,2:T(8,128)(2,1)}, u32[]{:S(2)}) copy-start(bf16[16,128,2,128]{1,0,3,2:T(8,128)(2,1)} %copy.9) | copy-start | bytes 3145732
  237.4 1.3 copy-start.1
  253.8 10.0 %slice-start.6 = ((s8[8388608]{0:T(1024)(128)(4,1)}), s8[4194304]{0:T(1024)(128)(4,1)S(1)}, s32[]{:S(2)}) async-start(s8[8388608]{0:T(1024)(128)(4,1)} %bitcast.120), calls=%async_computation.6 | async-start | bytes 8388608
  257.6 6.2 %slice-start.7 = ((s8[8388608]{0:T(1024)(128)(4,1)}), s8[4194304]{0:T(1024)(128)(4,1)S(1)}, s32[]{:S(2)}) async-start(s8[8388608]{0:T(1024)(128)(4,1)} %bitcast.120), calls=%async_computation.7 | async-start | bytes 8388608
  299.1 12.4 %slice-start = ((s8[16777216]{0:T(1024)(128)(4,1)}), s8[4194304]{0:T(1024)(128)(4,1)S(1)}, s32[]{:S(2)}) async-start(s8[16777216]{0:T(1024)(128)(4,1)} %bitcast.110), calls=%async_computation | async-start | bytes 8388608
  299.1 12.4 %slice-start.1 = ((s8[16777216]{0:T(1024)(128)(4,1)}), s8[4194304]{0:T(1024)(128)(4,1)S(1)}, s32[]{:S(2)}) async-start(s8[16777216]{0:T(1024)(128)(4,1)} %bitcast.110), calls=%async_computation.1 | async-start | bytes 8388608
  305.0 6.5 %slice-start.2 = ((s8[16777216]{0:T(1024)(128)(4,1)}), s8[4194304]{0:T(1024)(128)(4,1)S(1)}, s32[]{:S(2)}) async-start(s8[16777216]{0:T(1024)(128)(4,1)} %bitcast.110), calls=%async_computation.2 | async-start | bytes 8388608
  305.0 6.5 %slice-start.3 = ((s8[16777216]{0:T(1024)(128)(4,1)}), s8[4194304]{0:T(1024)(128)(4,1)S(1)}, s32[]{:S(2)}) async-start(s8[16777216]{0:T(1024)(128)(4,1)} %bitcast.110), calls=%async_computation.3 | async-start | bytes 8388608
  319.0 11.8 %slice-start.10 = ((s8[8388608]{0:T(1024)(128)(4,1)}), s8[4194304]{0:T(1024)(128)(4,1)S(1)}, s32[]{:S(2)}) async-start(s8[8388608]{0:T(1024)(128)(4,1)} %bitcast.131), calls=%async_computation.10 | async-start | bytes 8388608
  322.7 8.2 %slice-start.11 = ((s8[8388608]{0:T(1024)(128)(4,1)}), s8[4194304]{0:T(1024)(128)(4,1)S(1)}, s32[]{:S(2)}) async-start(s8[8388608]{0:T(1024)(128)(4,1)} %bitcast.131), calls=%async_computation.11 | async-start | bytes 8388608
  330.6 2.7 slice-start.8
  330.9 3.2 slice-start.9
  376.5 6.1 %copy-start.2 = (f32[2048,128]{1,0:T(8,128)S(1)}, f32[2048,128]{1,0:T(8,128)}, u32[]{:S(2)}) copy-start(f32[2048,128]{1,0:T(8,128)} %get-tuple-element.24) | copy-start | bytes 3145732
  376.5 6.1 %copy-start.3 = (f32[2048,128]{1,0:T(8,128)S(1)}, f32[2048,128]{1,0:T(8,128)}, u32[]{:S(2)}) copy-start(f32[2048,128]{1,0:T(8,128)} %get-tuple-element.40) | copy-start | bytes 3145732
